TPU v7x, 128 devices: a whole 4x4x4 slice. The times are simulated.
128 devices in a mesh: ctx: 16 (over y, x), tp: 8 (over z, core).
Axes of the slice: x: 4, y: 4, z: 4, core: 2. Of those that a mesh axis runs over, the one named last changes fastest.
Arguments:
- hidden: bfloat16 [8, 8192], P(None, 'ctx'), may hold values from -4.8 to 4.8, as said below
- norm_gains: bfloat16 [4, 8192], P(None, 'ctx'), may hold values from 0.5 to 1.5
- w_query: bfloat16 [4, 8192, 8192], P(None, 'ctx', 'tp'), may hold values from -0.0625 to 0.0625
- w_key: bfloat16 [4, 8192, 1024], P(None, 'ctx', 'tp'), may hold values from -0.125 to 0.125
- w_value: bfloat16 [4, 8192, 1024], P(None, 'ctx', 'tp'), may hold values from -0.125 to 0.125
- w_out: bfloat16 [4, 8192, 8192], P(None, 'tp', 'ctx'), may hold values from -0.0625 to 0.0625
- key_cache: bfloat16 [4, 8, 8, 2048, 128], P(None, None, 'tp', 'ctx'), may hold values from -9 to 9
- value_cache: bfloat16 [4, 8, 8, 2048, 128], P(None, None, 'tp', 'ctx'), may hold values from -6 to 6
- lengths: int32 [8], replicated, may hold values from 1 to 2048, 8200 in all
Outputs:
- updated: float32 [8, 8192], P(None, 'ctx')
Inputs may be any that keep to these rules, and one draw needn't show every extreme that they name: Each sequence has lengths[b] valid cache positions 0 .. lengths[b] - 1, between 1 and 2048; the longest sequence has exactly 2048; the new token sits at position lengths[b]. `hidden`: activations of order 0.2; in each block of 512 consecutive features one sequence, chosen at random, has entries four times larger.
All inputs are finite; a program needn't handle non-finite values.
Results may differ from a plain program's by a relative error of at most 0.02.
Values sent between devices are 32-bit elements.
A program may use at most 64 MiB of HBM per device.

v0:
```python
import functools
import math

import jax
import jax.numpy as jnp
from jax import lax
from jax.sharding import Mesh
from jax.sharding import PartitionSpec as P

D = 8192
CTX = ("ctx_0", "ctx_1")


mask_fill = -1e30
norm_eps = 1e-05
rope_base = 500000.0


def over_axes(shard, axes):
    return functools.reduce(lax.psum, axes, shard)


def one_axis_at_a_time(shard, axes):
    for axis in axes:
        shard = lax.pmax(shard, axis)
    return shard


def over_pieces(shard, axis):
    return lax.all_gather(shard, axis).sum(0)


def rotate(vectors, positions):
    width = vectors.shape[-1]
    half_width = width // 2
    exponents = jnp.arange(half_width, dtype=jnp.float32) * (2.0 / width)
    frequency = jnp.exp(-exponents * math.log(rope_base))
    angles = positions.astype(jnp.float32)[:, None] * frequency[None, :]
    cosine = jnp.cos(angles)[:, None, :]
    sine_part = jnp.sin(angles)[:, None, :]
    first_half = vectors[..., :half_width]
    second_half = vectors[..., half_width:]
    return jnp.concatenate(
        [
            first_half * cosine - second_half * sine_part,
            second_half * cosine + first_half * sine_part,
        ],
        axis=-1,
    )


def on_device(hidden, norm_gains, w_query, w_key, w_value, w_out, key_cache, value_cache, lengths):
    stream = hidden.astype(jnp.float32)
    seq_count = hidden.shape[0]
    head_width = key_cache.shape[4]
    location_total = key_cache.shape[3]
    kv_local = key_cache.shape[2]
    query_local = w_query.shape[2] // head_width
    group_size = query_local // kv_local
    logit_multiplier = 1.0 / math.sqrt(head_width)
    positions = lax.axis_index(CTX) * location_total + jnp.arange(location_total, dtype=jnp.int32)
    usable = (positions[None, :] < lengths[:, None])[:, None, None, :]
    for layer_idx in range(w_query.shape[0]):
        local_squares = jnp.sum(stream * stream, axis=1)
        scaled = (stream * norm_gains[layer_idx].astype(jnp.float32)).astype(jnp.bfloat16)
        query_part = jnp.dot(scaled, w_query[layer_idx], preferred_element_type=jnp.float32)
        key_part = jnp.dot(scaled, w_key[layer_idx], preferred_element_type=jnp.float32)
        value_part = jnp.dot(scaled, w_value[layer_idx], preferred_element_type=jnp.float32)
        squares = over_axes(local_squares, CTX)
        raw_query, raw_key, raw_value = (
            over_axes(query_part, CTX),
            over_axes(key_part, CTX),
            over_axes(value_part, CTX),
        )
        reciprocal_value = lax.rsqrt(squares / D + norm_eps)
        query = rotate(
            (raw_query * reciprocal_value[:, None]).reshape(seq_count, query_local, head_width),
            lengths,
        ).astype(jnp.bfloat16)
        fresh_lookup_vector = rotate(
            (raw_key * reciprocal_value[:, None]).reshape(seq_count, kv_local, head_width), lengths
        ).astype(jnp.bfloat16)
        new_value = (
            (raw_value * reciprocal_value[:, None])
            .reshape(seq_count, kv_local, head_width)
            .astype(jnp.bfloat16)
        )
        shared_head_sets = query.reshape(seq_count, kv_local, group_size, head_width)
        scores = (
            jnp.einsum(
                "bkgd,bksd->bkgs",
                shared_head_sets,
                key_cache[layer_idx],
                preferred_element_type=jnp.float32,
            )
            * logit_multiplier
        )
        masked = jnp.where(usable, scores, mask_fill)
        local_max = jnp.max(masked, axis=-1)
        attention_probabilities = jnp.where(usable, jnp.exp(masked - local_max[..., None]), 0.0)
        local_sum = jnp.sum(attention_probabilities, axis=-1)
        local_out = jnp.einsum(
            "bkgs,bksd->bkgd",
            attention_probabilities.astype(jnp.bfloat16),
            value_cache[layer_idx],
            preferred_element_type=jnp.float32,
        )
        largest = one_axis_at_a_time(local_max, CTX)
        factor = jnp.exp(local_max - largest)
        total_sum, total_out = (
            over_axes(local_sum * factor, CTX),
            over_axes(local_out * factor[..., None], CTX),
        )
        self_match_logit = (
            jnp.einsum(
                "uryj,urj->ury",
                shared_head_sets,
                fresh_lookup_vector,
                preferred_element_type=jnp.float32,
            )
            * logit_multiplier
        )
        row_top = jnp.maximum(largest, self_match_logit)
        carried = jnp.exp(largest - row_top)
        fresh = jnp.exp(self_match_logit - row_top)
        fresh_rounded = lax.optimization_barrier(fresh.astype(jnp.bfloat16)).astype(jnp.float32)
        numerator = (
            total_out * carried[..., None]
            + fresh_rounded[..., None] * new_value.astype(jnp.float32)[:, :, None, :]
        )
        denominator = total_sum * carried + fresh
        context = (
            (numerator / denominator[..., None])
            .reshape(seq_count, query_local * head_width)
            .astype(jnp.bfloat16)
        )
        head_part = jnp.dot(context, w_out[layer_idx], preferred_element_type=jnp.float32)
        stream = stream + over_pieces(head_part, "tp")
    return stream


def solution(mesh):
    finer = Mesh(mesh.devices.reshape(4, 4, mesh.shape["tp"]), ("ctx_0", "ctx_1", "tp"))
    return jax.shard_map(
        on_device,
        mesh=finer,
        in_specs=(
            P(None, CTX),
            P(None, CTX),
            P(None, CTX, "tp"),
            P(None, CTX, "tp"),
            P(None, CTX, "tp"),
            P(None, "tp", CTX),
            P(None, None, "tp", CTX, None),
            P(None, None, "tp", CTX, None),
            P(),
        ),
        out_specs=P(None, CTX),
        check_vma=False,
    )
```

profile of v0, /device:TPU:1, one launch (start us, length us, event | category | flops | bytes accessed | tf_op | source)
XLA Modules:
  0.0 402.6 jit_solution(12077693957421392516)
XLA Ops:
  5.5 1.5 fusion.22
  7.0 14.6 %all-reduce.15 = (f32[8,1024]{1,0:T(8,128)S(1)}, f32[8]{0:T(128)S(1)}) all-reduce(f32[8,1024]{1,0:T(8,128)S(1)} %fusion.22, f32[8]{0:T(128)S(1)} %fusion.65), channel_id=1, replica_groups=mesh['ctx_0'=4,'ctx_1'=4,'tp'=8] {'ctx_0'}, use_global_device_ids=true, to_apply=%region_0.0 | all-reduce | flops 8200 | bytes 65600 | tf_op jit(solution)/shard_map/psum | solution.py:20
  21.7 14.0 %all-reduce.7 = (f32[8,1024]{1,0:T(8,128)S(1)}, f32[8]{0:T(128)S(1)}) all-reduce(f32[8,1024]{1,0:T(8,128)S(1)} %get-tuple-element.51, f32[8]{0:T(128)S(1)} %get-tuple-element.52), channel_id=1, replica_groups=mesh['ctx_0'=4,'ctx_1'=4,'tp'=8] {'ctx_1'}, use_global_device_ids=true, to_apply=%region_1.0 | all-reduce | flops 8200 | bytes 65600 | tf_op jit(solution)/shard_map/psum | solution.py:20
  37.1 6.0 %pmax.56 = f32[8,1,8]{2,0,1:T(8,128)S(1)} all-reduce(f32[8,1,8]{2,0,1:T(8,128)S(1)} %bitcast.314), channel_id=1, replica_groups=mesh['ctx_0'=4,'ctx_1'=4,'tp'=8] {'ctx_0'}, use_global_device_ids=true, to_apply=%region_6.0 | all-reduce | flops 64 | bytes 512 | tf_op jit(solution)/shard_map/pmax | solution.py:25
  43.2 6.0 %pmax.57 = f32[8,1,8]{2,0,1:T(8,128)S(1)} all-reduce(f32[8,1,8]{2,0,1:T(8,128)S(1)} %pmax.56), channel_id=1, replica_groups=mesh['ctx_0'=4,'ctx_1'=4,'tp'=8] {'ctx_1'}, use_global_device_ids=true, to_apply=%region_7.0 | all-reduce | flops 64 | bytes 512 | tf_op jit(solution)/shard_map/pmax | solution.py:25
  50.5 12.8 %all-reduce.14 = (f32[8,1,8]{2,0,1:T(8,128)S(1)}, f32[8,128]{1,0:T(8,128)S(1)}, f32[8,128]{1,0:T(8,128)S(1)}, f32[8,1,8,128]{3,2,0,1:T(8,128)S(1)}) all-reduce(f32[8,1,8]{2,0,1:T(8,128)S(1)} %get-tuple-element.88, f32[8,128]{1,0:T(8,128)S(1)} %fusion.46, ...), channel_id=1, replica_groups=mesh['ctx_0'=4,'ctx_1'=4,'tp'=8] {'ctx_0'}, use_global_device_ids=true, to_apply=%region_15.16 | all-reduce | flops 10304 | bytes 82432 | tf_op jit(solution)/shard_map/psum | solution.py:20
  63.3 13.0 %all-reduce.6 = (f32[8,1,8]{2,0,1:T(8,128)S(1)}, f32[8,128]{1,0:T(8,128)S(1)}, f32[8,128]{1,0:T(8,128)S(1)}, f32[8,1,8,128]{3,2,0,1:T(8,128)S(1)}) all-reduce(f32[8,1,8]{2,0,1:T(8,128)S(1)} %get-tuple-element.47, f32[8,128]{1,0:T(8,128)S(1)} %get-tuple-element.48, ...), channel_id=1, replica_groups=mesh['ctx_0'=4,'ctx_1'=4,'tp'=8] {'ctx_1'}, use_global_device_ids=true, to_apply=%region_16.17 | all-reduce | flops 10304 | bytes 82432 | tf_op jit(solution)/shard_map/psum | solution.py:20
  78.4 32.6 %all-gather = f32[64,512]{1,0:T(8,128)S(1)} all-gather(f32[8,512]{1,0:T(8,128)S(1)} %fusion.20), channel_id=2, replica_groups=mesh['ctx_0'=4,'ctx_1'=4,'tp'=8] {'tp'}, dimensions={0}, use_global_device_ids=true | all-gather | bytes 147456 | tf_op jit(solution)/shard_map/all_gather | solution.py:30
  111.4 1.5 fusion.18
  112.9 11.5 %all-reduce.13 = (f32[8,1024]{1,0:T(8,128)S(1)}, f32[8]{0:T(128)S(1)}) all-reduce(f32[8,1024]{1,0:T(8,128)S(1)} %fusion.18, f32[8]{0:T(128)S(1)} %get-tuple-element.67), channel_id=1, replica_groups=mesh['ctx_0'=4,'ctx_1'=4,'tp'=8] {'ctx_0'}, use_global_device_ids=true, to_apply=%region_18.19 | all-reduce | flops 8200 | bytes 65600 | tf_op jit(solution)/shard_map/psum | solution.py:20
  124.4 11.2 %all-reduce.5 = (f32[8,1024]{1,0:T(8,128)S(1)}, f32[8]{0:T(128)S(1)}) all-reduce(f32[8,1024]{1,0:T(8,128)S(1)} %get-tuple-element.45, f32[8]{0:T(128)S(1)} %get-tuple-element.46), channel_id=1, replica_groups=mesh['ctx_0'=4,'ctx_1'=4,'tp'=8] {'ctx_1'}, use_global_device_ids=true, to_apply=%region_19.20 | all-reduce | flops 8200 | bytes 65600 | tf_op jit(solution)/shard_map/psum | solution.py:20
  136.1 7.6 %pmax.58 = f32[8,1,8]{2,0,1:T(8,128)S(1)} all-reduce(f32[8,1,8]{2,0,1:T(8,128)S(1)} %bitcast.315), channel_id=1, replica_groups=mesh['ctx_0'=4,'ctx_1'=4,'tp'=8] {'ctx_0'}, use_global_device_ids=true, to_apply=%region_24.25 | all-reduce | flops 64 | bytes 512 | tf_op jit(solution)/shard_map/pmax | solution.py:25
  143.7 7.6 %pmax.59 = f32[8,1,8]{2,0,1:T(8,128)S(1)} all-reduce(f32[8,1,8]{2,0,1:T(8,128)S(1)} %pmax.58), channel_id=1, replica_groups=mesh['ctx_0'=4,'ctx_1'=4,'tp'=8] {'ctx_1'}, use_global_device_ids=true, to_apply=%region_25.26 | all-reduce | flops 64 | bytes 512 | tf_op jit(solution)/shard_map/pmax | solution.py:25
  151.7 11.5 %all-reduce.12 = (f32[8,1,8]{2,0,1:T(8,128)S(1)}, f32[8,128]{1,0:T(8,128)S(1)}, f32[8,128]{1,0:T(8,128)S(1)}, f32[8,1,8,128]{3,2,0,1:T(8,128)S(1)}) all-reduce(f32[8,1,8]{2,0,1:T(8,128)S(1)} %get-tuple-element.83, f32[8,128]{1,0:T(8,128)S(1)} %fusion.42, ...), channel_id=1, replica_groups=mesh['ctx_0'=4,'ctx_1'=4,'tp'=8] {'ctx_0'}, use_global_device_ids=true, to_apply=%region_33.34 | all-reduce | flops 10304 | bytes 82432 | tf_op jit(solution)/shard_map/psum | solution.py:20
  163.3 11.7 %all-reduce.4 = (f32[8,1,8]{2,0,1:T(8,128)S(1)}, f32[8,128]{1,0:T(8,128)S(1)}, f32[8,128]{1,0:T(8,128)S(1)}, f32[8,1,8,128]{3,2,0,1:T(8,128)S(1)}) all-reduce(f32[8,1,8]{2,0,1:T(8,128)S(1)} %get-tuple-element.41, f32[8,128]{1,0:T(8,128)S(1)} %get-tuple-element.42, ...), channel_id=1, replica_groups=mesh['ctx_0'=4,'ctx_1'=4,'tp'=8] {'ctx_1'}, use_global_device_ids=true, to_apply=%region_34.35 | all-reduce | flops 10304 | bytes 82432 | tf_op jit(solution)/shard_map/psum | solution.py:20
  177.0 29.8 %all-gather.1 = f32[64,512]{1,0:T(8,128)S(1)} all-gather(f32[8,512]{1,0:T(8,128)S(1)} %fusion.16), channel_id=3, replica_groups=mesh['ctx_0'=4,'ctx_1'=4,'tp'=8] {'tp'}, dimensions={0}, use_global_device_ids=true | all-gather | bytes 147456 | tf_op jit(solution)/shard_map/all_gather | solution.py:30
  207.2 1.5 fusion.14
  208.7 12.7 %all-reduce.11 = (f32[8,1024]{1,0:T(8,128)S(1)}, f32[8]{0:T(128)S(1)}) all-reduce(f32[8,1024]{1,0:T(8,128)S(1)} %fusion.14, f32[8]{0:T(128)S(1)} %get-tuple-element.55), channel_id=1, replica_groups=mesh['ctx_0'=4,'ctx_1'=4,'tp'=8] {'ctx_0'}, use_global_device_ids=true, to_apply=%region_36.37 | all-reduce | flops 8200 | bytes 65600 | tf_op jit(solution)/shard_map/psum | solution.py:20
  221.4 12.6 %all-reduce.3 = (f32[8,1024]{1,0:T(8,128)S(1)}, f32[8]{0:T(128)S(1)}) all-reduce(f32[8,1024]{1,0:T(8,128)S(1)} %get-tuple-element.39, f32[8]{0:T(128)S(1)} %get-tuple-element.40), channel_id=1, replica_groups=mesh['ctx_0'=4,'ctx_1'=4,'tp'=8] {'ctx_1'}, use_global_device_ids=true, to_apply=%region_37.38 | all-reduce | flops 8200 | bytes 65600 | tf_op jit(solution)/shard_map/psum | solution.py:20
  234.6 6.1 %pmax.60 = f32[8,1,8]{2,0,1:T(8,128)S(1)} all-reduce(f32[8,1,8]{2,0,1:T(8,128)S(1)} %bitcast.316), channel_id=1, replica_groups=mesh['ctx_0'=4,'ctx_1'=4,'tp'=8] {'ctx_0'}, use_global_device_ids=true, to_apply=%region_42.43 | all-reduce | flops 64 | bytes 512 | tf_op jit(solution)/shard_map/pmax | solution.py:25
  240.7 6.2 %pmax.61 = f32[8,1,8]{2,0,1:T(8,128)S(1)} all-reduce(f32[8,1,8]{2,0,1:T(8,128)S(1)} %pmax.60), channel_id=1, replica_groups=mesh['ctx_0'=4,'ctx_1'=4,'tp'=8] {'ctx_1'}, use_global_device_ids=true, to_apply=%region_43.44 | all-reduce | flops 64 | bytes 512 | tf_op jit(solution)/shard_map/pmax | solution.py:25
  247.3 12.4 %all-reduce.10 = (f32[8,1,8]{2,0,1:T(8,128)S(1)}, f32[8,128]{1,0:T(8,128)S(1)}, f32[8,128]{1,0:T(8,128)S(1)}, f32[8,1,8,128]{3,2,0,1:T(8,128)S(1)}) all-reduce(f32[8,1,8]{2,0,1:T(8,128)S(1)} %get-tuple-element.78, f32[8,128]{1,0:T(8,128)S(1)} %fusion.38, ...), channel_id=1, replica_groups=mesh['ctx_0'=4,'ctx_1'=4,'tp'=8] {'ctx_0'}, use_global_device_ids=true, to_apply=%region_51.52 | all-reduce | flops 10304 | bytes 82432 | tf_op jit(solution)/shard_map/psum | solution.py:20
  259.7 13.2 %all-reduce.2 = (f32[8,1,8]{2,0,1:T(8,128)S(1)}, f32[8,128]{1,0:T(8,128)S(1)}, f32[8,128]{1,0:T(8,128)S(1)}, f32[8,1,8,128]{3,2,0,1:T(8,128)S(1)}) all-reduce(f32[8,1,8]{2,0,1:T(8,128)S(1)} %get-tuple-element.35, f32[8,128]{1,0:T(8,128)S(1)} %get-tuple-element.36, ...), channel_id=1, replica_groups=mesh['ctx_0'=4,'ctx_1'=4,'tp'=8] {'ctx_1'}, use_global_device_ids=true, to_apply=%region_52.53 | all-reduce | flops 10304 | bytes 82432 | tf_op jit(solution)/shard_map/psum | solution.py:20
  274.9 31.2 %all-gather.2 = f32[64,512]{1,0:T(8,128)S(1)} all-gather(f32[8,512]{1,0:T(8,128)S(1)} %fusion.12), channel_id=4, replica_groups=mesh['ctx_0'=4,'ctx_1'=4,'tp'=8] {'tp'}, dimensions={0}, use_global_device_ids=true | all-gather | bytes 147456 | tf_op jit(solution)/shard_map/all_gather | solution.py:30
  306.5 1.5 fusion.10
  308.0 11.5 %all-reduce.9 = (f32[8,1024]{1,0:T(8,128)S(1)}, f32[8]{0:T(128)S(1)}) all-reduce(f32[8,1024]{1,0:T(8,128)S(1)} %fusion.10, f32[8]{0:T(128)S(1)} %get-tuple-element.53), channel_id=1, replica_groups=mesh['ctx_0'=4,'ctx_1'=4,'tp'=8] {'ctx_0'}, use_global_device_ids=true, to_apply=%region_54.55 | all-reduce | flops 8200 | bytes 65600 | tf_op jit(solution)/shard_map/psum | solution.py:20
  319.5 11.2 %all-reduce.1 = (f32[8,1024]{1,0:T(8,128)S(1)}, f32[8]{0:T(128)S(1)}) all-reduce(f32[8,1024]{1,0:T(8,128)S(1)} %get-tuple-element.33, f32[8]{0:T(128)S(1)} %get-tuple-element.34), channel_id=1, replica_groups=mesh['ctx_0'=4,'ctx_1'=4,'tp'=8] {'ctx_1'}, use_global_device_ids=true, to_apply=%region_55.56 | all-reduce | flops 8200 | bytes 65600 | tf_op jit(solution)/shard_map/psum | solution.py:20
  331.2 7.7 %pmax.62 = f32[8,1,8]{2,0,1:T(8,128)S(1)} all-reduce(f32[8,1,8]{2,0,1:T(8,128)S(1)} %bitcast.313), channel_id=1, replica_groups=mesh['ctx_0'=4,'ctx_1'=4,'tp'=8] {'ctx_0'}, use_global_device_ids=true, to_apply=%region_60.61 | all-reduce | flops 64 | bytes 512 | tf_op jit(solution)/shard_map/pmax | solution.py:25
  338.9 7.3 %pmax.63 = f32[8,1,8]{2,0,1:T(8,128)S(1)} all-reduce(f32[8,1,8]{2,0,1:T(8,128)S(1)} %pmax.62), channel_id=1, replica_groups=mesh['ctx_0'=4,'ctx_1'=4,'tp'=8] {'ctx_1'}, use_global_device_ids=true, to_apply=%region_61.62 | all-reduce | flops 64 | bytes 512 | tf_op jit(solution)/shard_map/pmax | solution.py:25
  346.6 11.9 %all-reduce.8 = (f32[8,1,8]{2,0,1:T(8,128)S(1)}, f32[8,128]{1,0:T(8,128)S(1)}, f32[8,128]{1,0:T(8,128)S(1)}, f32[8,1,8,128]{3,2,0,1:T(8,128)S(1)}) all-reduce(f32[8,1,8]{2,0,1:T(8,128)S(1)} %get-tuple-element.73, f32[8,128]{1,0:T(8,128)S(1)} %fusion.34, ...), channel_id=1, replica_groups=mesh['ctx_0'=4,'ctx_1'=4,'tp'=8] {'ctx_0'}, use_global_device_ids=true, to_apply=%region_69.70 | all-reduce | flops 10304 | bytes 82432 | tf_op jit(solution)/shard_map/psum | solution.py:20
  358.4 11.2 %all-reduce = (f32[8,1,8]{2,0,1:T(8,128)S(1)}, f32[8,128]{1,0:T(8,128)S(1)}, f32[8,128]{1,0:T(8,128)S(1)}, f32[8,1,8,128]{3,2,0,1:T(8,128)S(1)}) all-reduce(f32[8,1,8]{2,0,1:T(8,128)S(1)} %get-tuple-element.29, f32[8,128]{1,0:T(8,128)S(1)} %get-tuple-element.30, ...), channel_id=1, replica_groups=mesh['ctx_0'=4,'ctx_1'=4,'tp'=8] {'ctx_1'}, use_global_device_ids=true, to_apply=%region_70.71 | all-reduce | flops 10304 | bytes 82432 | tf_op jit(solution)/shard_map/psum | solution.py:20
  371.7 30.3 %all-gather.3 = f32[64,512]{1,0:T(8,128)S(1)} all-gather(f32[8,512]{1,0:T(8,128)S(1)} %fusion.8), channel_id=5, replica_groups=mesh['ctx_0'=4,'ctx_1'=4,'tp'=8] {'tp'}, dimensions={0}, use_global_device_ids=true | all-gather | bytes 147456 | tf_op jit(solution)/shard_map/all_gather | solution.py:30
  (99 shorter events, 21.1 us)
Async XLA Ops:
  0.0 111.0 %copy-start.4 = (bf16[8,512]{1,0:T(8,128)(2,1)S(1)}, bf16[8,512]{1,0:T(8,128)(2,1)}, u32[]{:S(2)}) copy-start(bf16[8,512]{1,0:T(8,128)(2,1)} %param.9) | copy-start | bytes 24580
  0.0 111.2 %copy-start.2 = (bf16[4,512,128]{2,1,0:T(8,128)(2,1)S(1)}, bf16[4,512,128]{2,1,0:T(8,128)(2,1)}, u32[]{:S(2)}) copy-start(bf16[4,512,128]{2,1,0:T(8,128)(2,1)} %param.13) | copy-start | bytes 1572868
  0.0 111.3 %copy-start.3 = (bf16[4,512,128]{2,1,0:T(8,128)(2,1)S(1)}, bf16[4,512,128]{2,1,0:T(8,128)(2,1)}, u32[]{:S(2)}) copy-start(bf16[4,512,128]{2,1,0:T(8,128)(2,1)} %param.12) | copy-start | bytes 1572868
  0.0 151.5 %copy-start.1 = (bf16[4,8,1,128,128]{4,3,2,1,0:T(8,128)(2,1)S(1)}, bf16[4,8,1,128,128]{4,3,2,1,0:T(8,128)(2,1)}, u32[]{:S(2)}) copy-start(bf16[4,8,1,128,128]{4,3,2,1,0:T(8,128)(2,1)} %param.16) | copy-start | bytes 3145732
  0.0 135.8 %copy-start = (bf16[4,8,1,128,128]{4,3,2,1,0:T(8,128)(2,1)S(1)}, bf16[4,8,1,128,128]{4,3,2,1,0:T(8,128)(2,1)}, u32[]{:S(2)}) copy-start(bf16[4,8,1,128,128]{4,3,2,1,0:T(8,128)(2,1)} %param.15) | copy-start | bytes 3145732
where the time goes:
time: 404 us; the launch traced here: 403 us
  blocking collectives  375 us (93%)
  matrix products  19.7 us (5%)
  other arithmetic  7.17 us (2%)
    psum x16, blocking collectives, over_axes(): return functools.reduce(lax.psum, axes, shard)  197 us
    all_gather x4, blocking collectives, over_pieces(): return lax.all_gather(shard, axis).sum(0)  124 us
    pmax x8, blocking collectives, one_axis_at_a_time(): shard = lax.pmax(shard, axis)  54.4 us

commit v1 on v0

v1 whole, which is shorter than its diff:
```python
import functools
import math

import jax
import jax.numpy as jnp
from jax import lax
from jax.experimental import pallas as pl
from jax.experimental.pallas import tpu as pltpu
from jax.sharding import PartitionSpec as P

D = 8192
LAYERS = 4
BATCH = 8
HEADS = 8
HD = 128
FEATS = 512
POS = 128
NX = 4
NTP = 8
mask_fill = -1e30
norm_eps = 1e-05
rope_base = 500000.0
logit_multiplier = 1.0 / math.sqrt(HD)
T0, T1 = 6, 5
TB = 5


def kernel(
    hidden, gains, wq, wk, wv, wo, kc, vc, lengths,
    out,
    hid_s, gain_s, len_s, wq_s, wk_s, wv_s, wo_s, kc_s, vc_s,
    a0, a1, b0, b1, cbuf,
    load_sem, w_sem, a_send, a_recv, b_send, b_recv, c_send, c_recv,
):
    ctx = lax.axis_index("ctx")
    tp = lax.axis_index("tp")
    y = ctx // NX
    x = ctx % NX

    loads = [
        pltpu.make_async_copy(hidden, hid_s, load_sem.at[0]),
        pltpu.make_async_copy(gains, gain_s, load_sem.at[1]),
        pltpu.make_async_copy(lengths, len_s, load_sem.at[2]),
    ]
    for c in loads:
        c.start()
    weights = []
    for l in range(LAYERS):
        row = [
            pltpu.make_async_copy(src.at[l], dst.at[l], w_sem.at[l, i])
            for i, (src, dst) in enumerate(
                ((wq, wq_s), (wk, wk_s), (wv, wv_s), (kc, kc_s), (vc, vc_s), (wo, wo_s))
            )
        ]
        weights.append(row)
        for c in row:
            c.start()

    def along(axis, k):
        if axis == "x":
            return {"ctx": y * NX + (x + k) % NX}
        return {"ctx": ((y + k) % NX) * NX + x}

    barrier = pltpu.get_barrier_semaphore()
    for axis in ("x", "y"):
        for k in (2, 1, 3):
            pl.semaphore_signal(barrier, inc=1, device_id=along(axis, k))
    for k in range(1, NTP):
        pl.semaphore_signal(barrier, inc=1, device_id={"tp": (tp + k) % NTP})

    pending = []

    def exchange(buf, l, stage, axis, send, recv):
        copies = []
        for k in (2, 1, 3):
            c = pltpu.make_async_remote_copy(
                src_ref=buf.at[l, stage, 0],
                dst_ref=buf.at[l, stage, k],
                send_sem=send.at[l, stage, k],
                recv_sem=recv.at[l, stage, k],
                device_id=along(axis, k),
            )
            c.start()
            copies.append(c)
        pending.extend(copies)
        return copies

    def arrive(copies):
        for c in copies:
            c.wait_recv()

    for c in loads:
        c.wait()

    lane = lax.broadcasted_iota(jnp.int32, (BATCH, HD), 1)
    sub = lax.broadcasted_iota(jnp.int32, (BATCH, HD), 0)
    lens = jnp.full((BATCH, HD), len_s[0], jnp.int32)
    for b in range(1, BATCH):
        lens = jnp.where(sub == b, len_s[b], lens)
    exponents = (lane % (HD // 2)).astype(jnp.float32) * (2.0 / HD)
    angles = lens.astype(jnp.float32) * jnp.exp(-exponents * math.log(rope_base))
    cosine = jnp.cos(angles)
    sine = jnp.sin(angles)
    sine = jnp.where(lane < HD // 2, -sine, sine)
    usable = (ctx * POS + lane) < lens
    usable = jnp.concatenate([usable.astype(jnp.int32)] * HEADS, axis=0) > 0
    row_seq = lax.broadcasted_iota(jnp.int32, (HEADS * BATCH, HD), 0) % BATCH

    def tile(buf, l, stage, slot, t):
        return buf[l, stage, slot, pl.ds(t * 8, 8), :]

    def put(buf, l, stage, slot, t, value):
        buf[l, stage, slot, pl.ds(t * 8, 8), :] = value

    def summed(buf, l, stage, t):
        return (tile(buf, l, stage, 0, t) + tile(buf, l, stage, 1, t)) + (
            tile(buf, l, stage, 2, t) + tile(buf, l, stage, 3, t)
        )

    def spread(compact, j):
        return jnp.broadcast_to(compact[:, j : j + 1], (BATCH, HD))

    stream = hid_s[...].astype(jnp.float32)
    for l in range(LAYERS):
        squares = stream * stream
        squares = (squares[:, 0:128] + squares[:, 128:256]) + (
            squares[:, 256:384] + squares[:, 384:512]
        )
        put(a0, l, 0, 0, 5, squares)
        scaled = (stream * gain_s[l : l + 1, :].astype(jnp.float32)).astype(jnp.bfloat16)
        weights[l][0].wait()
        part = jnp.dot(scaled, wq_s[l, :, 0:640], preferred_element_type=jnp.float32)
        for t in range(5):
            put(a0, l, 0, 0, t, part[:, t * 128 : (t + 1) * 128])
        if l == 0:
            pl.semaphore_wait(barrier, 6 + NTP - 1)
        a0_1 = exchange(a0, l, 0, "x", a_send.at[0], a_recv.at[0])
        weights[l][1].wait()
        weights[l][2].wait()
        part = jnp.dot(scaled, wq_s[l, :, 640:1024], preferred_element_type=jnp.float32)
        key_part = jnp.dot(scaled, wk_s[l], preferred_element_type=jnp.float32)
        value_part = jnp.dot(scaled, wv_s[l], preferred_element_type=jnp.float32)
        for t in range(3):
            put(a1, l, 0, 0, t, part[:, t * 128 : (t + 1) * 128])
        put(a1, l, 0, 0, 3, key_part)
        put(a1, l, 0, 0, 4, value_part)
        a1_1 = exchange(a1, l, 0, "y", a_send.at[1], a_recv.at[1])
        arrive(a0_1)
        for t in range(T0):
            put(a0, l, 1, 0, t, summed(a0, l, 0, t))
        a0_2 = exchange(a0, l, 1, "y", a_send.at[0], a_recv.at[0])
        arrive(a1_1)
        for t in range(T1):
            put(a1, l, 1, 0, t, summed(a1, l, 0, t))
        a1_2 = exchange(a1, l, 1, "x", a_send.at[1], a_recv.at[1])

        weights[l][3].wait()
        weights[l][4].wait()
        arrive(a0_2)
        total = jnp.sum(summed(a0, l, 1, 5), axis=1, keepdims=True)
        inverse = lax.rsqrt(total / D + norm_eps)
        cos_l = cosine * inverse
        sin_l = sine * inverse

        def turn(u):
            return u * cos_l + pltpu.roll(u, HD // 2, 1) * sin_l

        heads = [turn(summed(a0, l, 1, t)) for t in range(5)]
        arrive(a1_2)
        heads += [turn(summed(a1, l, 1, t)) for t in range(3)]
        new_key = turn(summed(a1, l, 1, 3)).astype(jnp.bfloat16).astype(jnp.float32)
        new_value = (summed(a1, l, 1, 4) * inverse).astype(jnp.bfloat16).astype(jnp.float32)
        query = jnp.concatenate(heads, axis=0).astype(jnp.bfloat16)

        score = None
        for b in range(0, BATCH, 2):
            keys = kc_s[l, b : b + 2, 0].reshape(2 * POS, HD)
            both = lax.dot_general(
                query, keys, (((1,), (1,)), ((), ())), preferred_element_type=jnp.float32
            )
            first, second = both[:, :POS], both[:, POS:]
            score = first if score is None else jnp.where(row_seq == b, first, score)
            score = jnp.where(row_seq == b + 1, second, score)
        masked = jnp.where(usable, score * logit_multiplier, mask_fill)
        local_max = jnp.max(masked, axis=1, keepdims=True)
        weight = jnp.where(usable, jnp.exp(masked - local_max), 0.0)
        local_sum = jnp.sum(weight, axis=1, keepdims=True)
        rounded = weight.astype(jnp.bfloat16).astype(jnp.float32)
        wide = jnp.concatenate(
            [jnp.where(row_seq == b, rounded, 0.0).astype(jnp.bfloat16) for b in range(BATCH)],
            axis=1,
        )
        values = vc_s[l, :, 0].reshape(BATCH * POS, HD)
        local_out = jnp.dot(wide, values, preferred_element_type=jnp.float32)

        sends = []
        for half, buf in enumerate((b0, b1)):
            stats = jnp.zeros((BATCH, HD), jnp.float32)
            for j in range(4):
                h = half * 4 + j
                rows = slice(h * 8, h * 8 + 8)
                put(buf, l, 0, 0, j, local_out[rows])
                stats = jnp.where(lane == j, local_max[rows], stats)
                stats = jnp.where(lane == 4 + j, local_sum[rows], stats)
            put(buf, l, 0, 0, 4, stats)
            sends.append(
                exchange(buf, l, 0, "xy"[half], b_send.at[half], b_recv.at[half])
            )

        own = [jnp.zeros((BATCH, HD), jnp.float32)] * 2
        for h in range(HEADS):
            rounded_head = heads[h].astype(jnp.bfloat16).astype(jnp.float32)
            dots = jnp.sum(rounded_head * new_key, axis=1, keepdims=True) * logit_multiplier
            own[h // 4] = jnp.where(lane == h % 4, dots, own[h // 4])

        def factors(buf, stage):
            stats = [tile(buf, l, stage, s, 4) for s in range(4)]
            top = jnp.maximum(
                jnp.maximum(stats[0], stats[1]), jnp.maximum(stats[2], stats[3])
            )
            scale = [jnp.exp(s - top) for s in stats]
            sums = [s * pltpu.roll(f, 4, 1) for s, f in zip(stats, scale)]
            return top, scale, (sums[0] + sums[1]) + (sums[2] + sums[3])

        second = []
        for half, buf in enumerate((b0, b1)):
            arrive(sends[half])
            top, scale, sums = factors(buf, 0)
            for j in range(4):
                merged = [tile(buf, l, 0, s, j) * spread(scale[s], j) for s in range(4)]
                put(buf, l, 1, 0, j, (merged[0] + merged[1]) + (merged[2] + merged[3]))
            put(buf, l, 1, 0, 4, jnp.where(lane < 4, top, jnp.where(lane < 8, sums, 0.0)))
            second.append(
                exchange(buf, l, 1, "yx"[half], b_send.at[half], b_recv.at[half])
            )

        weights[l][5].wait()
        contribution = None
        for half, buf in enumerate((b0, b1)):
            arrive(second[half])
            top, scale, sums = factors(buf, 1)
            row_top = jnp.maximum(top, own[half])
            carried = jnp.exp(top - row_top)
            fresh = jnp.exp(own[half] - row_top)
            denominator = pltpu.roll(sums, HD - 4, 1) * carried + fresh
            denominator = jnp.where(lane < 4, denominator, 1.0)
            carried = carried / denominator
            fresh = fresh.astype(jnp.bfloat16).astype(jnp.float32) / denominator
            scale = [s * carried for s in scale]
            context = []
            for j in range(4):
                merged = [tile(buf, l, 1, s, j) * spread(scale[s], j) for s in range(4)]
                context.append(
                    (merged[0] + merged[1])
                    + (merged[2] + merged[3])
                    + spread(fresh, j) * new_value
                )
            context = jnp.concatenate(context, axis=1).astype(jnp.bfloat16)
            term = jnp.dot(
                context,
                wo_s[l, half * 512 : (half + 1) * 512, :],
                preferred_element_type=jnp.float32,
            )
            contribution = term if contribution is None else contribution + term
        cbuf[l, pl.ds(tp, 1)] = jnp.concatenate(
            [contribution[:, t * 128 : (t + 1) * 128] for t in range(4)], axis=0
        )[None]
        copies = []
        for k in (4, 5, 3, 2, 6, 1, 7):
            c = pltpu.make_async_remote_copy(
                src_ref=cbuf.at[l, tp],
                dst_ref=cbuf.at[l, tp],
                send_sem=c_send.at[l, k],
                recv_sem=c_recv.at[l, k],
                device_id={"tp": (tp + k) % NTP},
            )
            c.start()
            copies.append(c)
        pending.extend(copies)
        arrive(copies)
        tiles = []
        for t in range(4):
            terms = [cbuf[l, s, pl.ds(t * 8, 8), :] for s in range(NTP)]
            tiles.append(
                ((terms[0] + terms[1]) + (terms[2] + terms[3]))
                + ((terms[4] + terms[5]) + (terms[6] + terms[7]))
            )
        stream = stream + jnp.concatenate(tiles, axis=1)

    out[...] = stream
    for c in pending:
        c.wait_send()


def on_device(*args):
    hbm = pl.BlockSpec(memory_space=pl.ANY)
    f32, bf16 = jnp.float32, jnp.bfloat16
    dma = pltpu.SemaphoreType.DMA
    return pl.pallas_call(
        kernel,
        out_shape=jax.ShapeDtypeStruct((BATCH, FEATS), f32),
        in_specs=[hbm] * 9,
        out_specs=pl.BlockSpec(memory_space=pltpu.VMEM),
        scratch_shapes=[
            pltpu.VMEM((BATCH, FEATS), bf16),
            pltpu.VMEM((LAYERS, FEATS), bf16),
            pltpu.SMEM((BATCH,), jnp.int32),
            pltpu.VMEM((LAYERS, FEATS, HEADS * HD), bf16),
            pltpu.VMEM((LAYERS, FEATS, HD), bf16),
            pltpu.VMEM((LAYERS, FEATS, HD), bf16),
            pltpu.VMEM((LAYERS, HEADS * HD, FEATS), bf16),
            pltpu.VMEM((LAYERS, BATCH, 1, POS, HD), bf16),
            pltpu.VMEM((LAYERS, BATCH, 1, POS, HD), bf16),
            pltpu.VMEM((LAYERS, 2, NX, T0 * 8, HD), f32),
            pltpu.VMEM((LAYERS, 2, NX, T1 * 8, HD), f32),
            pltpu.VMEM((LAYERS, 2, NX, TB * 8, HD), f32),
            pltpu.VMEM((LAYERS, 2, NX, TB * 8, HD), f32),
            pltpu.VMEM((LAYERS, NTP, 4 * 8, HD), f32),
            dma((3,)),
            dma((LAYERS, 6)),
            dma((2, LAYERS, 2, NX)),
            dma((2, LAYERS, 2, NX)),
            dma((2, LAYERS, 2, NX)),
            dma((2, LAYERS, 2, NX)),
            dma((LAYERS, NTP)),
            dma((LAYERS, NTP)),
        ],
        compiler_params=pltpu.CompilerParams(collective_id=0, has_side_effects=True),
    )(*args)


def solution(mesh):
    return jax.shard_map(
        on_device,
        mesh=mesh,
        in_specs=(
            P(None, "ctx"),
            P(None, "ctx"),
            P(None, "ctx", "tp"),
            P(None, "ctx", "tp"),
            P(None, "ctx", "tp"),
            P(None, "tp", "ctx"),
            P(None, None, "tp", "ctx", None),
            P(None, None, "tp", "ctx", None),
            P(),
        ),
        out_specs=P(None, "ctx"),
        check_vma=False,
    )
```

time: 404 us -> 94.5 us (0.23)
  blocking collectives: 375 us -> 0 us
  Pallas kernels: 0 us -> 93 us
  matrix products: 19.7 us -> 0 us
  other arithmetic: 7.17 us -> 0 us
    psum x16 -> x0, blocking collectives: 197 us -> none  [over_axes(): return functools.reduce(lax.psum, axes, shard)]
    all_gather x4 -> x0, blocking collectives: 124 us -> none  [over_pieces(): return lax.all_gather(shard, axis).sum(0)]
    pallas_call x0 -> x1, Pallas kernels: none -> 93 us  [on_device(): pl.pallas_call(kernel, out_shape=jax.ShapeDtypeStruct((BATCH, FEATS), f32...]
    pmax x8 -> x0, blocking collectives: 54.4 us -> none  [one_axis_at_a_time(): shard = lax.pmax(shard, axis)]
    dot_general x28 -> x0, matrix products: 19.7 us -> none  [the longest x4 5.92 us: on_device(): jnp.dot(scaled, w_query[layer_idx], preferred_element_type=jnp.float32)]
where the time goes in v1:
time: 94.5 us; the launch traced here: 94.3 us
  Pallas kernels  93 us (98%)
  local copies, waits for them, and re-layouts  1.32 us (1%)
    pallas_call x1, Pallas kernels, on_device(): pl.pallas_call(kernel, out_shape=jax.ShapeDtypeStruct((BATCH, FEATS), f32...  93 us

profile of v1, /device:TPU:1, one launch (start us, length us, event | category | flops | bytes accessed | tf_op | source)
XLA Modules:
  0.0 94.3 jit_solution(9894470308875080031)
XLA Ops:
  0.0 93.0 %shard_map.91 = f32[8,512]{1,0:T(8,128)} custom-call(bf16[8,512]{1,0:T(8,128)(2,1)} %hidden.1, bf16[4,512]{1,0:T(4,128)(2,1)} %gains.1, bf16[4,512,1024]{2,1,0:T(8,128)(2,1)} %wq.1, bf16[4,512,128]{2,1,0:T(8,128)(2,1)} %wk.1, bf16[4,512,128]{2,1,0:T(8,128)(2,1)} %wv.1, bf16[4,1024,512]{2,1,0:T(8,128)(2,1)} %wo.1, bf16[4,8,1,128,128]{4,3,2,1,0:T(8,128)(2,1)} %kc.1, ...), custom_call_target="tpu_custom_call" | custom-call | tf_op jit(solution)/shard_map/pallas_call | solution.py:299
  93.0 1.3 %copy.11 = f32[8,512]{1,0:T(8,128)} copy(f32[8,512]{1,0:T(8,128)} %shard_map.91) | data formatting | bytes 32768
